TPU v7x, 32 devices: a whole 2x2x4 slice. The times are simulated.
32 devices in a mesh: rows: 8 (over z, y), trees: 4 (over x, core).
Axes of the slice: x: 2, y: 2, z: 4, core: 2. Of those that a mesh axis runs over, the one named last changes fastest.
Arguments:
- node_of_row: int32 [4, 16384], P('trees', 'rows'), may hold values from 0 to 63
- bag_weight: int32 [4, 16384], P('trees', 'rows'), may hold values from 0 to 6, as said below
- smaller_side: int32 [4, 32], P('trees'), may hold values from 0 to 1
- bins: int32 [16384, 256], P('rows'), may hold values from 0 to 31
- target: float32 [16384], P('rows'), may hold values from -6 to 6
- parent_hist: float32 [4, 256, 3072], P('trees', 'rows')
Outputs:
- child_hist: float32 [4, 256, 6144], P('trees', 'rows')
- best_gain: float32 [4, 64], P('trees')
- importance: float32 [256], P('rows')
Inputs may be any that keep to these rules, and one draw needn't show every extreme that they name: `bag_weight`: poisson weights with mean one.
All inputs are finite; a program needn't handle non-finite values.
Results may differ from a plain program's by a relative error of at most 0.002.
Values sent between devices are 32-bit elements; how exact they have to be, the bound alone decides.
A program may use at most 64 MiB of HBM per device.

v0:
```python
import functools
import math

import jax
import jax.numpy as jnp
from jax import lax
from jax.experimental import pallas as pl
from jax.experimental.pallas import tpu as pltpu
from jax.sharding import PartitionSpec as P

BINS = 32
MESH = pl.DeviceIdType.MESH
HIGH = lax.Precision.HIGHEST
NT = (((1,), (1,)), ((), ()))


def kernel(
    R, T, owned, nbins, pairs, nrows,
    node_ref, wgt_ref, flag_ref, bins_ref, target_ref, parent_ref,
    acc_ref, best_ref, imp_ref,
    node_v, wgt_v, bins_v, sendbuf, recv, stat_v, par_v, acc, hot, spread, tn_v, sg_v, msg_b, got_b, msg_i, got_i,
    in_sem, out_sem, d_send, d_recv, s_send, s_recv, y_send, x_send, x_recv, p_send, p_recv, q_send, q_recv,
    b_send, b_recv, i_send, i_recv,
):
    f32, bf16, i32 = jnp.float32, jnp.bfloat16, jnp.int32
    r = lax.axis_index("rows")
    t = lax.axis_index("trees")
    tp = t + 1 - 2 * lax.rem(t, 2)
    tx = lax.rem(t + T // 2, T)
    tpx = lax.rem(tp + T // 2, T)
    quarter = nrows // T
    width = 6 * pairs

    bins_in = pltpu.make_async_copy(
        bins_ref.at[pl.ds(pl.multiple_of(t * quarter, quarter), quarter), :], bins_v, in_sem.at[0]
    )
    bins_in.start()
    node_in = pltpu.make_async_copy(node_ref, node_v, in_sem.at[2])
    wgt_in = pltpu.make_async_copy(wgt_ref, wgt_v, in_sem.at[3])
    target_in = pltpu.make_async_copy(target_ref, stat_v.at[r, :, pl.ds(2 * nrows, nrows)], in_sem.at[4])
    node_in.start()
    wgt_in.start()
    target_in.start()
    par_in = pltpu.make_async_copy(parent_ref, par_v, in_sem.at[1])
    par_in.start()

    barrier = pltpu.get_barrier_semaphore()
    for off in range(1, R):
        pl.semaphore_signal(barrier, inc=1, device_id=(lax.rem(r + off, R), t), device_id_type=MESH)
    for off in range(1, T):
        pl.semaphore_signal(barrier, inc=1, device_id=(r, lax.rem(t + off, T)), device_id_type=MESH)

    node_in.wait()
    wgt_in.wait()
    target_in.wait()
    stat_v[r, :, 0:nrows] = node_v[...].astype(f32)
    stat_v[r, :, nrows : 2 * nrows] = wgt_v[...].astype(f32)
    bins_in.wait()
    sendbuf[...] = bins_v[...].astype(f32).T.reshape(R, owned, quarter)
    recv[r, t] = sendbuf[r]

    def flip(m):
        peer, bit = r, 1
        while bit < R:
            on = lax.rem(m // bit, 2)
            peer = peer + on * bit * (1 - 2 * lax.rem(r // bit, 2))
            bit *= 2
        return peer

    def direct(m, src):
        return pltpu.make_async_remote_copy(
            sendbuf.at[flip(m)],
            recv.at[src, t],
            d_send.at[m],
            d_recv.at[src],
            device_id=(flip(m), t),
            device_id_type=MESH,
        )

    def stats(src, to, send):
        return pltpu.make_async_remote_copy(
            stat_v.at[src], stat_v.at[src], send.at[src], s_recv.at[src], device_id=(to, t), device_id_type=MESH
        )

    def stats_out(m):
        return pltpu.make_async_remote_copy(
            stat_v.at[r], stat_v.at[r], s_send.at[m], s_recv.at[r], device_id=(flip(m), t), device_id_type=MESH
        )

    def relay(src, slot, to, send, got):
        return pltpu.make_async_remote_copy(
            recv.at[src, slot], recv.at[src, slot], send.at[src], got.at[src], device_id=(r, to), device_id_type=MESH
        )

    pl.semaphore_wait(barrier, R + T - 2)

    relay(r, t, tx, x_send, x_recv).start()
    relay(r, t, tp, p_send, p_recv).start()

    def launch(m, _):
        @pl.when((m == 1) | (lax.rem(m, 2) == 0))
        def _():
            stats_out(m).start()

        direct(m, r).start()
        return 0

    lax.fori_loop(1, R, launch, 0)

    flag = flag_ref[...].astype(f32)
    c_row = lax.broadcasted_iota(i32, (width, pairs), 0)
    p_col = lax.broadcasted_iota(i32, (width, pairs), 1)
    side_c = jnp.sum(jnp.where(c_row // 6 == p_col, flag, 0.0), axis=1, keepdims=True)
    c_one = lax.broadcasted_iota(i32, (width, 1), 0)
    kid_c = (lax.rem(c_one, 6) // 3).astype(f32)
    node_c = 2.0 * (c_one // 6).astype(f32) + side_c
    sign_c = jnp.where(kid_c == side_c, 1.0, -1.0)
    tn_v[...] = jnp.broadcast_to(node_c, (width, quarter)).astype(bf16)
    sg_v[...] = jnp.broadcast_to(sign_c, (width, quarter)).astype(bf16)
    group = 4
    deep = group * 3 * pairs
    e_row = lax.broadcasted_iota(i32, (width, deep), 1)
    e_col = lax.broadcasted_iota(i32, (width, deep), 0)
    par_in.wait()
    stack = jnp.concatenate(
        [par_v[0, :, g * deep : (g + 1) * deep] for g in range(nbins // group)], axis=0
    )
    for k in range(group):
        want = k * 3 * pairs + 3 * (e_col // 6) + lax.rem(e_col, 3)
        pick = jnp.where((e_row == want) & (sign_c < 0.0), 1.0, 0.0)
        spreadout = lax.dot_general(stack, pick, NT, precision=HIGH, preferred_element_type=f32)
        for g in range(nbins // group):
            b = g * group + k
            acc[b * owned : (b + 1) * owned, :] = spreadout[g * owned : (g + 1) * owned, :]

    third = lax.rem(lax.broadcasted_iota(i32, (48, quarter), 0), 3)

    def piece(src, slot):
        base = pl.multiple_of(slot * quarter, quarter)
        nodes = stat_v[src, :, pl.ds(base, quarter)]
        w = stat_v[src, :, pl.ds(pl.multiple_of(base + nrows, quarter), quarter)]
        y = stat_v[src, :, pl.ds(pl.multiple_of(base + 2 * nrows, quarter), quarter)]
        wy = w * y
        wyy = wy * y
        stat = jnp.where(third == 0, w, jnp.where(third == 1, wy, wyy)).astype(bf16)
        node = jnp.broadcast_to(nodes, (48, quarter)).astype(bf16)
        for g in range(width // 48):
            at = slice(g * 48, (g + 1) * 48)
            spread[at, :] = jnp.where(node == tn_v[at, :], stat, jnp.zeros_like(stat)) * sg_v[at, :]
        cols = recv[src, slot].astype(bf16)
        for b in range(nbins):
            hot[b * owned : (b + 1) * owned, :] = jnp.where(
                cols == jnp.asarray(b, bf16), jnp.ones_like(cols), jnp.zeros_like(cols)
            )
        acc[...] += lax.dot_general(hot[...], spread[...], NT, preferred_element_type=f32)

    def step(i, _):
        @pl.when((i >= 1) & (i < R))
        def _():
            src = flip(i)
            direct(i, src).wait_recv()
            relay(src, t, tx, x_send, x_recv).start()
            relay(src, t, tp, p_send, p_recv).start()
            stats(src, src, y_send).wait_recv()

            @pl.when(lax.rem(i, 2) == 0)
            def _():
                stats(src, flip(1), y_send).start()

        def part(k, _):
            lag = (k + 1) // 2
            src = flip(i - lag)
            slot = jnp.where(k == 0, t, jnp.where(k == 1, tx, jnp.where(k == 2, tp, tpx)))
            live = (i >= lag) & (i < R + lag)

            @pl.when(live & (k == 1))
            def _():
                relay(src, tx, tx, x_send, x_recv).wait_recv()
                relay(src, tx, tp, q_send, q_recv).start()

            @pl.when(live & (k == 2))
            def _():
                relay(src, tp, tp, p_send, p_recv).wait_recv()

            @pl.when(live & (k == 3))
            def _():
                relay(src, tpx, tp, q_send, q_recv).wait_recv()

            @pl.when(live)
            def _():
                piece(src, slot)

            return 0

        lax.fori_loop(0, T, part, 0)
        return 0

    lax.fori_loop(0, R + 2, step, 0)

    acc_out = pltpu.make_async_copy(acc, acc_ref, out_sem.at[0])
    acc_out.start()

    def at(b):
        return acc[b * owned : (b + 1) * owned, :]

    total = at(0)
    for b in range(1, nbins):
        total = total + at(b)

    def shift(x):
        return jnp.concatenate([x[:, 1:], x[:, :1]], axis=1)

    s_all = shift(total)
    cum = jnp.zeros((owned, width), f32)
    top = jnp.full((owned, width), -jnp.inf, f32)
    for b in range(nbins - 1):
        cum = cum + at(b)
        s = shift(cum)
        o = s_all - s
        g = s * s / (jnp.maximum(cum, 0.0) + 1.0)
        g = g + o * o / (jnp.maximum(total - cum, 0.0) + 1.0)
        top = jnp.maximum(top, g)
    top = top - s_all * s_all / (jnp.maximum(total, 0.0) + 1.0)
    lane = lax.broadcasted_iota(i32, (owned, width), 1)
    top = jnp.where(lax.rem(lane, 3) == 0, top, 0.0)
    mine = jnp.max(top, axis=0, keepdims=True)
    n_i = lax.broadcasted_iota(i32, (2 * pairs, width), 0)
    c_i = lax.broadcasted_iota(i32, (2 * pairs, width), 1)
    take = jnp.where(c_i == 3 * n_i, 1.0, 0.0)
    best = lax.dot_general(
        jnp.broadcast_to(mine, (8, width)), take, NT, precision=HIGH, preferred_element_type=f32
    )
    summed = lax.dot_general(jnp.ones((8, width), f32), top, NT, precision=HIGH, preferred_element_type=f32)
    msg_b[:, 0 : 2 * pairs] = best
    msg_i[:, 0:owned] = summed
    got_b[r] = msg_b[...]
    got_i[t] = msg_i[...]

    def tell_b(off):
        peer = lax.rem(r + off, R)
        return pltpu.make_async_remote_copy(
            msg_b, got_b.at[r], b_send.at[off], b_recv.at[r], device_id=(peer, t), device_id_type=MESH
        )

    def tell_i(off):
        peer = lax.rem(t + off, T)
        return pltpu.make_async_remote_copy(
            msg_i, got_i.at[t], i_send.at[off], i_recv.at[t], device_id=(r, peer), device_id_type=MESH
        )

    for off in range(1, R):
        tell_b(off).start()
    for off in range(1, T):
        tell_i(off).start()

    def drain(m, _):
        direct(m, r).wait_send()

        @pl.when((m == 1) | (lax.rem(m, 2) == 0))
        def _():
            stats_out(m).wait_send()

        @pl.when(lax.rem(m, 2) == 0)
        def _():
            stats(flip(m), flip(1), y_send).wait_send()

        return 0

    lax.fori_loop(1, R, drain, 0)

    def drain_relay(s, _):
        relay(s, t, tx, x_send, x_recv).wait_send()
        relay(s, t, tp, p_send, p_recv).wait_send()
        relay(s, tx, tp, q_send, q_recv).wait_send()
        return 0

    lax.fori_loop(0, R, drain_relay, 0)

    for off in range(1, T):
        src = lax.rem(t - off + T, T)
        pltpu.make_async_remote_copy(
            msg_i, got_i.at[src], i_send.at[off], i_recv.at[src], device_id=(r, src), device_id_type=MESH
        ).wait_recv()
    for off in range(1, R):
        src = lax.rem(r - off + R, R)
        pltpu.make_async_remote_copy(
            msg_b, got_b.at[src], b_send.at[off], b_recv.at[src], device_id=(src, t), device_id_type=MESH
        ).wait_recv()
    peak = got_b[0]
    for s in range(1, R):
        peak = jnp.maximum(peak, got_b[s])
    best_ref[...] = peak[0:1, 0 : 2 * pairs]
    tally = got_i[0]
    for s in range(1, T):
        tally = tally + got_i[s]
    imp_ref[...] = tally[0:1, 0:owned] / (T * 2 * pairs)
    for off in range(1, T):
        tell_i(off).wait_send()
    for off in range(1, R):
        tell_b(off).wait_send()
    acc_out.wait()


def layout(owned, nbins, width, acc_ref, best_in, imp_in, child_ref, best_ref, imp_ref):
    for j in range(nbins // 2):
        a0 = acc_ref[2 * j * owned : (2 * j + 1) * owned, :]
        a1 = acc_ref[(2 * j + 1) * owned : (2 * j + 2) * owned, :]
        child_ref[0, :, 2 * j * width : (2 * j + 2) * width] = jnp.concatenate([a0, a1], axis=1)
    best_ref[...] = best_in[...]
    imp_ref[...] = imp_in[...]


def fused(R, T, node_of_row, bag_weight, smaller_side, bins, target, parent_hist):
    nrows, feat = bins.shape
    pairs = smaller_side.shape[1]
    owned = feat // R
    quarter = nrows // T
    width = 6 * pairs
    f32, bf16 = jnp.float32, jnp.bfloat16
    vmem = pl.BlockSpec(memory_space=pltpu.VMEM)
    hbm = pl.BlockSpec(memory_space=pl.ANY)
    dma = pltpu.SemaphoreType.DMA
    acc, best, imp = pl.pallas_call(
        functools.partial(kernel, R, T, owned, BINS, pairs, nrows),
        out_shape=(
            jax.ShapeDtypeStruct((BINS * owned, width), f32),
            jax.ShapeDtypeStruct((1, 2 * pairs), f32),
            jax.ShapeDtypeStruct((1, owned), f32),
        ),
        in_specs=[hbm, hbm, vmem, hbm, hbm, hbm],
        out_specs=(hbm, vmem, vmem),
        scratch_shapes=[
            pltpu.VMEM((1, nrows), jnp.int32),
            pltpu.VMEM((1, nrows), jnp.int32),
            pltpu.VMEM((quarter, feat), jnp.int32),
            pltpu.VMEM((R, owned, quarter), f32),
            pltpu.VMEM((R, T, owned, quarter), f32),
            pltpu.VMEM((R, 1, 3 * nrows), f32),
            pltpu.VMEM((1, owned, BINS * 3 * pairs), f32),
            pltpu.VMEM((BINS * owned, width), f32),
            pltpu.VMEM((BINS * owned, quarter), bf16),
            pltpu.VMEM((width, quarter), bf16),
            pltpu.VMEM((width, quarter), bf16),
            pltpu.VMEM((width, quarter), bf16),
            pltpu.VMEM((8, 128), f32),
            pltpu.VMEM((R, 8, 128), f32),
            pltpu.VMEM((8, 128), f32),
            pltpu.VMEM((T, 8, 128), f32),
            dma((5,)), dma((1,)), dma((R,)),
            dma((R,)), dma((R,)), dma((R,)), dma((R,)),
            dma((R,)), dma((R,)), dma((R,)), dma((R,)), dma((R,)), dma((R,)),
            dma((R,)), dma((R,)), dma((T,)), dma((T,)),
        ],
        compiler_params=pltpu.CompilerParams(collective_id=0, has_side_effects=True),
    )(node_of_row, bag_weight, smaller_side, bins, target.reshape(1, nrows), parent_hist)
    parts = 4
    rows, lanes = BINS // parts * owned, BINS // parts * width
    whole = lambda n: pl.BlockSpec((1, n), lambda i: (0, 0))
    child, best, imp = pl.pallas_call(
        functools.partial(layout, owned, BINS // parts, width),
        grid=(parts,),
        out_shape=(
            jax.ShapeDtypeStruct((1, owned, BINS * width), f32),
            jax.ShapeDtypeStruct((1, 2 * pairs), f32),
            jax.ShapeDtypeStruct((1, owned), f32),
        ),
        in_specs=[pl.BlockSpec((rows, width), lambda i: (i, 0)), whole(2 * pairs), whole(owned)],
        out_specs=(pl.BlockSpec((1, owned, lanes), lambda i: (0, 0, i)), whole(2 * pairs), whole(owned)),
    )(acc, best, imp)
    return child, best, imp.reshape(owned)


def plain(node_of_row, bag_weight, smaller_side, bins, target, parent_hist):
    nrows = bins.shape[0]
    feat = bins.shape[1]
    pairs = smaller_side.shape[1]
    nbins = BINS
    nodes = node_of_row[0]
    flags = smaller_side[0]
    pair = nodes // 2
    side = nodes % 2
    pair_hot = pair[:, None] == jnp.arange(pairs, dtype=jnp.int32)[None, :]
    flag_row = jnp.sum(jnp.where(pair_hot, flags[None, :], 0), axis=1)
    keep = (side == flag_row).astype(jnp.float32)
    wk = bag_weight[0].astype(jnp.float32) * keep
    stats = jnp.stack([wk, wk * target, wk * target * target], axis=1).astype(jnp.bfloat16)
    spread = (pair_hot.astype(jnp.bfloat16)[:, :, None] * stats[:, None, :]).reshape(nrows, pairs * 3)
    levels = jnp.arange(nbins, dtype=jnp.int32)
    owned = feat // lax.axis_size("rows")
    width = math.gcd(lax.axis_size("rows") * owned, 32)

    def one_block(index):
        cols = lax.dynamic_slice_in_dim(bins, index * width, width, 1)
        onehot = (
            (cols[:, :, None] == levels[None, None, :]).astype(jnp.bfloat16).reshape(nrows, width * nbins)
        )
        part = jnp.einsum("rk,rm->km", onehot, spread, preferred_element_type=jnp.float32)
        return part.reshape(width, nbins * pairs * 3)

    blocks = lax.map(one_block, jnp.arange(lax.axis_size("rows") * owned // width, dtype=jnp.int32))
    small = lax.psum_scatter(
        blocks.reshape(lax.axis_size("rows") * owned, nbins * pairs * 3), "rows", scatter_dimension=0, tiled=True
    )
    small = small.reshape(owned, nbins, pairs, 3)
    parent = parent_hist[0].reshape(owned, nbins, pairs, 3)
    sibling = parent - small
    take = jnp.arange(2, dtype=jnp.int32)[None, :] == flags[:, None]
    children = jnp.where(take[None, None, :, :, None], small[:, :, :, None, :], sibling[:, :, :, None, :])
    children = children.reshape(owned, nbins, 2 * pairs, 3)
    ccum = jnp.cumsum(children[..., 0], axis=1)
    scum = jnp.cumsum(children[..., 1], axis=1)
    call = ccum[:, -1:, :]
    sall = scum[:, -1:, :]
    left_c = ccum[:, :-1, :]
    left_s = scum[:, :-1, :]
    gain = left_s * left_s / (jnp.maximum(left_c, 0.0) + 1.0)
    gain = gain + (sall - left_s) ** 2 / (jnp.maximum(call - left_c, 0.0) + 1.0)
    gain = gain - sall * sall / (jnp.maximum(call, 0.0) + 1.0)
    fgain = jnp.max(gain, axis=1)
    best = lax.pmax(jnp.max(fgain, axis=0), "rows")
    featsum = lax.psum(jnp.sum(fgain, axis=1), "trees")
    importance = featsum / (lax.axis_size("trees") * node_of_row.shape[0] * 2 * pairs)
    child_hist = children.reshape(owned, nbins * 2 * pairs * 3)
    return (child_hist[None], best[None], importance)


def solution(mesh):
    R, T = mesh.shape["rows"], mesh.shape["trees"]

    def shards(node_of_row, bag_weight, smaller_side, bins, target, parent_hist):
        nrows, feat = bins.shape
        pairs = smaller_side.shape[1]
        owned = feat // R
        fits = T == 4 and R % 2 == 0 and R & (R - 1) == 0 and node_of_row.shape[0] == 1
        fits = fits and owned % 16 == 0 and owned <= 128 and nrows % (T * 128) == 0
        fits = fits and pairs % 32 == 0 and pairs <= 64 and R * nrows * owned * 4 <= 4 << 20
        body = functools.partial(fused, R, T) if fits else plain
        return body(node_of_row, bag_weight, smaller_side, bins, target, parent_hist)

    return jax.shard_map(
        shards,
        mesh=mesh,
        in_specs=(
            P("trees", "rows"),
            P("trees", "rows"),
            P("trees", None),
            P("rows", None),
            P("rows"),
            P("trees", "rows", None),
        ),
        out_specs=(P("trees", "rows", None), P("trees", None), P("rows")),
        check_vma=False,
    )
```

profile of v0, /device:TPU:0, one launch (start us, length us, event | category | flops | bytes accessed | tf_op | source)
XLA Modules:
  0.0 41.5 jit_solution(9949538875622508043)
XLA Ops:
  0.6 37.4 %shard_map.85 = (f32[1024,192]{1,0:T(8,128)}, f32[1,64]{1,0:T(1,128)}, f32[1,32]{1,0:T(1,128)}) custom-call(s32[1,2048]{1,0:T(1,128)} %node_ref.1, s32[1,2048]{1,0:T(1,128)} %wgt_ref.1, s32[1,32]{1,0:T(1,128)} %flag_ref.1, s32[2048,256]{1,0:T(8,128)} %bins_ref.1, f32[1,2048]{1,0:T(1,128)} %bitcast.2, f32[1,32,3072]{2,1,0:T(8,128)} %parent_ref.1), custom_call_target="tpu_custom_call" | custom-call | tf_op jit(solution)/shard_map/pallas_call | solution.py:323
  38.0 3.5 %shard_map.86 = (f32[1,32,6144]{2,1,0:T(8,128)}, f32[1,64]{1,0:T(1,128)}, f32[1,32]{1,0:T(1,128)}) custom-call(f32[1024,192]{1,0:T(8,128)} %get-tuple-element.9.acc_ref, f32[1,64]{1,0:T(1,128)} %get-tuple-element.10.best_in, f32[1,32]{1,0:T(1,128)} %get-tuple-element.11.imp_in), custom_call_target="tpu_custom_call" | custom-call | tf_op jit(solution)/shard_map/pallas_call | solution.py:359
where the time goes:
time: 41.7 us; the launch traced here: 41.5 us
  Pallas kernels  40.9 us (98%)
  between operations  0.64 us (2%)
    pallas_call x1, Pallas kernels, fused(): pl.pallas_call(functools.partial(kernel, R, T, owned, BINS, pairs, nrows)...  37.4 us
    pallas_call x1, Pallas kernels, fused(): pl.pallas_call(functools.partial(layout, owned, BINS // parts, width), gr...  3.49 us

commit v1 on v0

v1 whole, which is shorter than its diff:
```python
import functools
import math

import jax
import jax.numpy as jnp
from jax import lax
from jax.experimental import pallas as pl
from jax.experimental.pallas import tpu as pltpu
from jax.sharding import PartitionSpec as P

BINS = 32
MESH = pl.DeviceIdType.MESH
HIGH = lax.Precision.HIGHEST
NT = (((1,), (1,)), ((), ()))


def kernel(
    R, T, owned, nbins, pairs, nrows,
    node_ref, wgt_ref, flag_ref, bins_ref, target_ref, parent_ref,
    child_ref, small_ref,
    *scratch,
):
    rows = nbins // 4 * owned
    acc = pltpu.ACC
    spec = lambda q, m: acc(q)((m, 256), jnp.float32)
    pl.run_scoped(
        functools.partial(
            body, R, T, owned, nbins, pairs, nrows,
            node_ref, wgt_ref, flag_ref, bins_ref, target_ref, parent_ref, child_ref, small_ref, *scratch
        ),
        spec(0, rows), spec(0, rows), spec(1, rows), spec(1, rows), spec(0, 16), spec(1, 16),
    )


def body(
    R, T, owned, nbins, pairs, nrows,
    node_ref, wgt_ref, flag_ref, bins_ref, target_ref, parent_ref,
    child_ref, small_ref,
    node_v, wgt_v, flag_v, bins_v, own_v, own_t, sendbuf, recv, stat_v, par_v, acc, spread, tn_v, sg_v,
    msg_b, got_b, msg_i, got_i,
    in_sem, d_send, d_recv, s_send, s_recv, y_send, x_send, x_recv, p_send, p_recv, q_send, q_recv,
    b_send, b_recv, i_send, i_recv,
    acc0, acc1, acc2, acc3, idle0, idle1,
):
    f32, bf16, i32 = jnp.float32, jnp.bfloat16, jnp.int32
    accs = (acc0, acc1, acc2, acc3)
    r = lax.axis_index("rows")
    t = lax.axis_index("trees")
    tp = t + 1 - 2 * lax.rem(t, 2)
    tx = lax.rem(t + T // 2, T)
    tpx = lax.rem(tp + T // 2, T)
    quarter = nrows // T
    width = 6 * pairs
    groups = nbins // 4

    bins_in = pltpu.make_async_copy(
        bins_ref.at[pl.ds(pl.multiple_of(t * quarter, quarter), quarter), :], bins_v, in_sem.at[0]
    )
    bins_in.start()
    node_in = pltpu.make_async_copy(node_ref, node_v, in_sem.at[2])
    wgt_in = pltpu.make_async_copy(wgt_ref, wgt_v, in_sem.at[3])
    target_in = pltpu.make_async_copy(target_ref, stat_v.at[r, :, pl.ds(2 * nrows, nrows)], in_sem.at[4])
    node_in.start()
    wgt_in.start()
    target_in.start()
    flag_in = pltpu.make_async_copy(flag_ref, flag_v, in_sem.at[5])
    flag_in.start()
    own_in = pltpu.make_async_copy(
        bins_ref.at[:, pl.ds(pl.multiple_of(r * owned // 128 * 128, 128), 128)], own_v, in_sem.at[6]
    )
    own_in.start()
    par_in = pltpu.make_async_copy(parent_ref, par_v, in_sem.at[1])
    par_in.start()

    barrier = pltpu.get_barrier_semaphore()
    for off in range(1, R):
        pl.semaphore_signal(barrier, inc=1, device_id=(lax.rem(r + off, R), t), device_id_type=MESH)
    for off in range(1, T):
        pl.semaphore_signal(barrier, inc=1, device_id=(r, lax.rem(t + off, T)), device_id_type=MESH)

    node_in.wait()
    wgt_in.wait()
    target_in.wait()
    stat_v[r, :, 0:nrows] = node_v[...].astype(f32)
    stat_v[r, :, nrows : 2 * nrows] = wgt_v[...].astype(f32)
    bins_in.wait()
    sendbuf[...] = bins_v[...].astype(f32).T.reshape(R, owned, quarter)

    def flip(m):
        peer, bit = r, 1
        while bit < R:
            on = lax.rem(m // bit, 2)
            peer = peer + on * bit * (1 - 2 * lax.rem(r // bit, 2))
            bit *= 2
        return peer

    def direct(m, src):
        return pltpu.make_async_remote_copy(
            sendbuf.at[flip(m)],
            recv.at[src, t],
            d_send.at[m],
            d_recv.at[src],
            device_id=(flip(m), t),
            device_id_type=MESH,
        )

    def stats(src, to, send):
        return pltpu.make_async_remote_copy(
            stat_v.at[src], stat_v.at[src], send.at[src], s_recv.at[src], device_id=(to, t), device_id_type=MESH
        )

    def stats_out(m):
        return pltpu.make_async_remote_copy(
            stat_v.at[r], stat_v.at[r], s_send.at[m], s_recv.at[r], device_id=(flip(m), t), device_id_type=MESH
        )

    def relay(src, slot, to, send, got):
        return pltpu.make_async_remote_copy(
            recv.at[src, slot], recv.at[src, slot], send.at[src], got.at[src], device_id=(r, to), device_id_type=MESH
        )

    pl.semaphore_wait(barrier, R + T - 2)

    def launch(m, _):
        @pl.when((m == 1) | (lax.rem(m, 2) == 0))
        def _():
            stats_out(m).start()

        direct(m, r).start()
        return 0

    lax.fori_loop(1, R, launch, 0)

    for a in accs:
        acc[0] = pltpu.matmul_pop(a)
    child_ref[0, 0:16, 0:256] = pltpu.matmul_pop(idle0)
    child_ref[0, 0:16, 0:256] = pltpu.matmul_pop(idle1)
    flag_in.wait()
    flag = flag_v[...].astype(f32)
    c_row = lax.broadcasted_iota(i32, (width, pairs), 0)
    p_col = lax.broadcasted_iota(i32, (width, pairs), 1)
    side_c = jnp.sum(jnp.where(c_row // 6 == p_col, flag, 0.0), axis=1, keepdims=True)
    c_one = lax.broadcasted_iota(i32, (width, 1), 0)
    kid_c = (lax.rem(c_one, 6) // 3).astype(f32)
    node_c = 2.0 * (c_one // 6).astype(f32) + side_c
    sign_c = jnp.where(kid_c == side_c, 1.0, -1.0)
    tn_v[...] = jnp.broadcast_to(node_c, (width, quarter)).astype(bf16)
    sg_v[...] = jnp.broadcast_to(sign_c, (width, quarter)).astype(bf16)
    spread[width:, :] = jnp.zeros((256 - width, quarter), bf16)

    own_in.wait()
    lead = pl.multiple_of(lax.rem(r * owned, 128), owned)
    for q in range(T):
        own_t[q] = own_v[q * quarter : (q + 1) * quarter, :].astype(f32).T
        recv[r, q] = own_t[q, pl.ds(lead, owned), :]

    deep = 12 * pairs
    e_lane = lax.broadcasted_iota(i32, (width, 256), 1)
    e_col = lax.broadcasted_iota(i32, (width, 256), 0)
    par_in.wait()
    for k in range(4):
        base = k // 2 * 128
        want = k * 3 * pairs - base + 3 * (e_col // 6) + lax.rem(e_col, 3)
        pick = jnp.where((e_lane == want) & (sign_c < 0.0), 1.0, 0.0).astype(bf16)
        pick = jnp.concatenate([pick, jnp.zeros((256 - width, 256), bf16)], axis=0)
        pltpu.matmul_push_rhs(pick, staging_register=0, mxu_index=k // 2, transpose=True)
        rest = jnp.concatenate(
            [par_v[0, :, g * deep + base : g * deep + base + 256] for g in range(groups)], axis=0
        )
        for limb in range(3):
            part = rest.astype(bf16)
            pltpu.matmul_acc_lhs(accs[k], part, load_staged_rhs=0 if limb == 0 else None)
            rest = rest - part.astype(f32)

    third = lax.rem(lax.broadcasted_iota(i32, (48, quarter), 0), 3)
    count = R * T

    def place(e):
        u = e - T
        idx = u + jnp.where(u >= 1, 3, 0) + jnp.where(u >= 4, 1, 0)
        idx = idx + jnp.where(u >= 4 * R - 8, 1, 0) + jnp.where(u >= 4 * R - 5, 3, 0)
        k = lax.rem(idx, 4)
        m = idx // 4 + 1 - (k + 1) // 2
        m = jnp.where(e < T, 0, m)
        slot = jnp.where(k == 0, t, jnp.where(k == 1, tx, jnp.where(k == 2, tp, tpx)))
        slot = jnp.where(e < T, e, slot)
        k = jnp.where(e < T, -1, k)
        return m, k, slot

    def lay(src, slot):
        base = pl.multiple_of(slot * quarter, quarter)
        nodes = stat_v[src, :, pl.ds(base, quarter)]
        w = stat_v[src, :, pl.ds(pl.multiple_of(base + nrows, quarter), quarter)]
        y = stat_v[src, :, pl.ds(pl.multiple_of(base + 2 * nrows, quarter), quarter)]
        wy = w * y
        wyy = wy * y
        stat = jnp.where(third == 0, w, jnp.where(third == 1, wy, wyy)).astype(bf16)
        node = jnp.broadcast_to(nodes, (48, quarter)).astype(bf16)
        for g in range(width // 48):
            at = slice(g * 48, (g + 1) * 48)
            spread[at, :] = jnp.where(node == tn_v[at, :], stat, jnp.zeros_like(stat)) * sg_v[at, :]

    def stage(tile, q):
        pltpu.matmul_push_rhs(
            spread[:, tile * 256 : (tile + 1) * 256], staging_register=tile, mxu_index=q, transpose=True
        )

    lay(r, 0)
    for tile in range(2):
        for q in range(2):
            stage(tile, q)

    def step(e, _):
        m, k, slot = place(e)
        src = flip(m)

        @pl.when(k == 0)
        def _():
            direct(m, src).wait_recv()
            relay(src, t, tx, x_send, x_recv).start()
            relay(src, t, tp, p_send, p_recv).start()

        @pl.when(k == 1)
        def _():
            relay(src, tx, tx, x_send, x_recv).wait_recv()
            relay(src, tx, tp, q_send, q_recv).start()

        @pl.when(k == 2)
        def _():
            relay(src, tp, tp, p_send, p_recv).wait_recv()

        @pl.when(k == 3)
        def _():
            relay(src, tpx, tp, q_send, q_recv).wait_recv()

        m2, k2, slot2 = place(jnp.minimum(e + 1, count - 1))
        src2 = flip(m2)

        @pl.when((k2 == 0) & (e + 1 < count))
        def _():
            stats(src2, src2, y_send).wait_recv()

            @pl.when(lax.rem(m2, 2) == 0)
            def _():
                stats(src2, flip(1), y_send).start()

        lay(src2, slot2)
        cols = recv[src, slot].astype(bf16)
        for tile in range(2):
            c = cols[:, tile * 256 : (tile + 1) * 256]
            for j in range(2):
                for q in range(2):
                    a = 2 * q + j
                    hot = jnp.concatenate(
                        [
                            jnp.where(c == jnp.asarray(4 * g + a, bf16), jnp.ones_like(c), jnp.zeros_like(c))
                            for g in range(groups)
                        ],
                        axis=0,
                    )
                    pltpu.matmul_acc_lhs(accs[a], hot, load_staged_rhs=tile if j == 0 else None)
                    if j == 0:
                        stage(tile, q)
        return 0

    lax.fori_loop(0, count, step, 0)
    nothing = jnp.zeros((16, 256), bf16)
    for tile in range(2):
        pltpu.matmul_acc_lhs(idle0, nothing, load_staged_rhs=tile)
        pltpu.matmul_acc_lhs(idle1, nothing, load_staged_rhs=tile)
    for k in range(4):
        acc[k] = pltpu.matmul_pop(accs[k])
    msg_i[...] = pltpu.matmul_pop(idle0)[0:1, 0:128] + pltpu.matmul_pop(idle1)[0:1, 0:128]

    def at(b, h):
        return acc[b % 4, b // 4 * owned : (b // 4 + 1) * owned, h * 128 : (h + 1) * 128]

    def shift(x):
        return pltpu.roll(x, 127, 1)

    lane = lax.broadcasted_iota(i32, (owned, 128), 1)
    per_feature = jnp.zeros((owned, 1), f32)
    for h in range(2):
        total = at(0, h)
        for b in range(1, nbins):
            total = total + at(b, h)
        s_all = shift(total)
        cum = jnp.zeros((owned, 128), f32)
        top = jnp.full((owned, 128), -jnp.inf, f32)
        for b in range(nbins - 1):
            cum = cum + at(b, h)
            s = shift(cum)
            o = s_all - s
            g = s * s / (jnp.maximum(cum, 0.0) + 1.0)
            g = g + o * o / (jnp.maximum(total - cum, 0.0) + 1.0)
            top = jnp.maximum(top, g)
        top = top - s_all * s_all / (jnp.maximum(total, 0.0) + 1.0)
        at_lane = lane + h * 128
        fits = (lax.rem(at_lane, 3) == 0) & (at_lane < width)
        msg_b[:, h * 128 : (h + 1) * 128] = jnp.max(jnp.where(fits, top, -jnp.inf), axis=0, keepdims=True)
        per_feature = per_feature + jnp.sum(jnp.where(fits, top, 0.0), axis=1, keepdims=True)
    msg_i[...] = jnp.broadcast_to(per_feature, (owned, 128)).T[0:1, :] if owned == 128 else jnp.concatenate(
        [jnp.broadcast_to(per_feature, (owned, 128)).T[0:1, :], jnp.zeros((1, 128 - owned), f32)], axis=1
    )
    got_b[r] = msg_b[...]
    got_i[t] = msg_i[...]

    def tell_b(off):
        peer = lax.rem(r + off, R)
        return pltpu.make_async_remote_copy(
            msg_b, got_b.at[r], b_send.at[off], b_recv.at[r], device_id=(peer, t), device_id_type=MESH
        )

    def tell_i(off):
        peer = lax.rem(t + off, T)
        return pltpu.make_async_remote_copy(
            msg_i, got_i.at[t], i_send.at[off], i_recv.at[t], device_id=(r, peer), device_id_type=MESH
        )

    for off in range(1, R):
        tell_b(off).start()
    for off in range(1, T):
        tell_i(off).start()

    low = lane < 64
    for j in range(nbins // 2):
        base = 2 * j * width
        mid, end = pltpu.roll(at(2 * j + 1, 0), 64, 1), pltpu.roll(at(2 * j + 1, 1), 64, 1)
        child_ref[0, :, base : base + 128] = at(2 * j, 0)
        child_ref[0, :, base + 128 : base + 256] = jnp.where(low, at(2 * j, 1), mid)
        child_ref[0, :, base + 256 : base + 384] = jnp.where(low, mid, end)

    def drain(m, _):
        src = flip(m)
        direct(m, r).wait_send()

        @pl.when((m == 1) | (lax.rem(m, 2) == 0))
        def _():
            stats_out(m).wait_send()

        @pl.when(lax.rem(m, 2) == 0)
        def _():
            stats(src, flip(1), y_send).wait_send()

        relay(src, t, tx, x_send, x_recv).wait_send()
        relay(src, t, tp, p_send, p_recv).wait_send()
        relay(src, tx, tp, q_send, q_recv).wait_send()
        return 0

    lax.fori_loop(1, R, drain, 0)

    for off in range(1, T):
        src = lax.rem(t - off + T, T)
        pltpu.make_async_remote_copy(
            msg_i, got_i.at[src], i_send.at[off], i_recv.at[src], device_id=(r, src), device_id_type=MESH
        ).wait_recv()
    for off in range(1, R):
        src = lax.rem(r - off + R, R)
        pltpu.make_async_remote_copy(
            msg_b, got_b.at[src], b_send.at[off], b_recv.at[src], device_id=(src, t), device_id_type=MESH
        ).wait_recv()
    peak = got_b[0]
    for s in range(1, R):
        peak = jnp.maximum(peak, got_b[s])
    small_ref[:, 0:256] = peak
    tally = got_i[0]
    for s in range(1, T):
        tally = tally + got_i[s]
    small_ref[:, 256:384] = tally / (T * 2 * pairs)
    for off in range(1, T):
        tell_i(off).wait_send()
    for off in range(1, R):
        tell_b(off).wait_send()


def finish(owned, pairs, child_in, small_in, child_ref, best_ref, imp_ref, sem):
    out = pltpu.make_async_copy(child_in, child_ref, sem)
    out.start()
    width = 6 * pairs
    n_i = lax.broadcasted_iota(jnp.int32, (2 * pairs, width), 0)
    c_i = lax.broadcasted_iota(jnp.int32, (2 * pairs, width), 1)
    take = jnp.where(c_i == 3 * n_i, 1.0, 0.0)
    held = lax.rem(lax.broadcasted_iota(jnp.int32, (8, width), 1), 3) == 0
    peak = jnp.where(held, jnp.broadcast_to(small_in[:, 0:width], (8, width)), 0.0)
    best = lax.dot_general(peak, take, NT, precision=HIGH, preferred_element_type=jnp.float32)
    best_ref[...] = best[0:1, :]
    imp_ref[...] = small_in[:, 256 : 256 + owned]
    out.wait()


def fused(R, T, node_of_row, bag_weight, smaller_side, bins, target, parent_hist):
    nrows, feat = bins.shape
    pairs = smaller_side.shape[1]
    owned = feat // R
    quarter = nrows // T
    width = 6 * pairs
    f32, bf16 = jnp.float32, jnp.bfloat16
    vmem = pl.BlockSpec(memory_space=pltpu.VMEM)
    hbm = pl.BlockSpec(memory_space=pl.ANY)
    dma = pltpu.SemaphoreType.DMA
    child, small = pl.pallas_call(
        functools.partial(kernel, R, T, owned, BINS, pairs, nrows),
        out_shape=(pltpu.VMEM((1, owned, BINS * width), f32), pltpu.VMEM((1, 384), f32)),
        in_specs=[hbm, hbm, hbm, hbm, hbm, hbm],
        out_specs=(vmem, vmem),
        scratch_shapes=[
            pltpu.VMEM((1, nrows), jnp.int32),
            pltpu.VMEM((1, nrows), jnp.int32),
            pltpu.VMEM((1, pairs), jnp.int32),
            pltpu.VMEM((quarter, feat), jnp.int32),
            pltpu.VMEM((nrows, 128), jnp.int32),
            pltpu.VMEM((T, 128, quarter), f32),
            pltpu.VMEM((R, owned, quarter), f32),
            pltpu.VMEM((R, T, owned, quarter), f32),
            pltpu.VMEM((R, 1, 3 * nrows), f32),
            pltpu.VMEM((1, owned, BINS * 3 * pairs), f32),
            pltpu.VMEM((4, BINS // 4 * owned, 256), f32),
            pltpu.VMEM((256, quarter), bf16),
            pltpu.VMEM((width, quarter), bf16),
            pltpu.VMEM((width, quarter), bf16),
            pltpu.VMEM((1, 256), f32),
            pltpu.VMEM((R, 1, 256), f32),
            pltpu.VMEM((1, 128), f32),
            pltpu.VMEM((T, 1, 128), f32),
            dma((7,)), dma((R,)),
            dma((R,)), dma((R,)), dma((R,)), dma((R,)),
            dma((R,)), dma((R,)), dma((R,)), dma((R,)), dma((R,)), dma((R,)),
            dma((R,)), dma((R,)), dma((T,)), dma((T,)),
        ],
        compiler_params=pltpu.CompilerParams(collective_id=0, has_side_effects=True),
    )(*[pltpu.with_memory_space_constraint(x, pltpu.HBM) for x in (node_of_row, bag_weight, smaller_side, bins, target.reshape(1, nrows), parent_hist)])
    child, best, imp = pl.pallas_call(
        functools.partial(finish, owned, pairs),
        out_shape=(
            jax.ShapeDtypeStruct((1, owned, BINS * width), f32),
            jax.ShapeDtypeStruct((1, 2 * pairs), f32),
            jax.ShapeDtypeStruct((1, owned), f32),
        ),
        in_specs=[vmem, vmem],
        out_specs=(hbm, vmem, vmem),
        scratch_shapes=[dma],
        compiler_params=pltpu.CompilerParams(vmem_limit_bytes=8 << 20),
    )(pltpu.with_memory_space_constraint(child, pltpu.VMEM), pltpu.with_memory_space_constraint(small, pltpu.VMEM))
    return child, best, imp.reshape(owned)


def plain(node_of_row, bag_weight, smaller_side, bins, target, parent_hist):
    nrows = bins.shape[0]
    feat = bins.shape[1]
    pairs = smaller_side.shape[1]
    nbins = BINS
    nodes = node_of_row[0]
    flags = smaller_side[0]
    pair = nodes // 2
    side = nodes % 2
    pair_hot = pair[:, None] == jnp.arange(pairs, dtype=jnp.int32)[None, :]
    flag_row = jnp.sum(jnp.where(pair_hot, flags[None, :], 0), axis=1)
    keep = (side == flag_row).astype(jnp.float32)
    wk = bag_weight[0].astype(jnp.float32) * keep
    stats = jnp.stack([wk, wk * target, wk * target * target], axis=1).astype(jnp.bfloat16)
    spread = (pair_hot.astype(jnp.bfloat16)[:, :, None] * stats[:, None, :]).reshape(nrows, pairs * 3)
    levels = jnp.arange(nbins, dtype=jnp.int32)
    owned = feat // lax.axis_size("rows")
    width = math.gcd(lax.axis_size("rows") * owned, 32)

    def one_block(index):
        cols = lax.dynamic_slice_in_dim(bins, index * width, width, 1)
        onehot = (
            (cols[:, :, None] == levels[None, None, :]).astype(jnp.bfloat16).reshape(nrows, width * nbins)
        )
        part = jnp.einsum("rk,rm->km", onehot, spread, preferred_element_type=jnp.float32)
        return part.reshape(width, nbins * pairs * 3)

    blocks = lax.map(one_block, jnp.arange(lax.axis_size("rows") * owned // width, dtype=jnp.int32))
    small = lax.psum_scatter(
        blocks.reshape(lax.axis_size("rows") * owned, nbins * pairs * 3), "rows", scatter_dimension=0, tiled=True
    )
    small = small.reshape(owned, nbins, pairs, 3)
    parent = parent_hist[0].reshape(owned, nbins, pairs, 3)
    sibling = parent - small
    take = jnp.arange(2, dtype=jnp.int32)[None, :] == flags[:, None]
    children = jnp.where(take[None, None, :, :, None], small[:, :, :, None, :], sibling[:, :, :, None, :])
    children = children.reshape(owned, nbins, 2 * pairs, 3)
    ccum = jnp.cumsum(children[..., 0], axis=1)
    scum = jnp.cumsum(children[..., 1], axis=1)
    call = ccum[:, -1:, :]
    sall = scum[:, -1:, :]
    left_c = ccum[:, :-1, :]
    left_s = scum[:, :-1, :]
    gain = left_s * left_s / (jnp.maximum(left_c, 0.0) + 1.0)
    gain = gain + (sall - left_s) ** 2 / (jnp.maximum(call - left_c, 0.0) + 1.0)
    gain = gain - sall * sall / (jnp.maximum(call, 0.0) + 1.0)
    fgain = jnp.max(gain, axis=1)
    best = lax.pmax(jnp.max(fgain, axis=0), "rows")
    featsum = lax.psum(jnp.sum(fgain, axis=1), "trees")
    importance = featsum / (lax.axis_size("trees") * node_of_row.shape[0] * 2 * pairs)
    child_hist = children.reshape(owned, nbins * 2 * pairs * 3)
    return (child_hist[None], best[None], importance)


def solution(mesh):
    R, T = mesh.shape["rows"], mesh.shape["trees"]

    def shards(node_of_row, bag_weight, smaller_side, bins, target, parent_hist):
        nrows, feat = bins.shape
        pairs = smaller_side.shape[1]
        owned = feat // R
        fits = T == 4 and R % 2 == 0 and R & (R - 1) == 0 and node_of_row.shape[0] == 1
        fits = fits and R >= 4 and owned in (16, 32) and feat % 128 == 0 and nrows == T * 512
        fits = fits and pairs == 32 and R * nrows * owned * 4 <= 4 << 20
        body = functools.partial(fused, R, T) if fits else plain
        return body(node_of_row, bag_weight, smaller_side, bins, target, parent_hist)

    return jax.shard_map(
        shards,
        mesh=mesh,
        in_specs=(
            P("trees", "rows"),
            P("trees", "rows"),
            P("trees", None),
            P("rows", None),
            P("rows"),
            P("trees", "rows", None),
        ),
        out_specs=(P("trees", "rows", None), P("trees", None), P("rows")),
        check_vma=False,
    )
```

time: 41.7 us -> 37.4 us (0.90)
  Pallas kernels: 40.9 us -> 36.6 us
    pallas_call x1, Pallas kernels: 37.4 us -> 35.2 us  [fused(): pl.pallas_call(functools.partial(kernel, R, T, owned, BINS, pairs, nrows)...]
    pallas_call x1, Pallas kernels: 3.49 us -> 1.4 us  [fused(): pl.pallas_call(functools.partial(finish, owned, pairs), out_shape=(jax.Sh...]
where the time goes in v1:
time: 37.4 us; the launch traced here: 37.3 us
  Pallas kernels  36.6 us (98%)
  between operations  0.64 us (2%)
    pallas_call x1, Pallas kernels, fused(): pl.pallas_call(functools.partial(kernel, R, T, owned, BINS, pairs, nrows)...  35.2 us
    pallas_call x1, Pallas kernels, fused(): pl.pallas_call(functools.partial(finish, owned, pairs), out_shape=(jax.Sh...  1.4 us

profile of v1, /device:TPU:0, one launch (start us, length us, event | category | flops | bytes accessed | tf_op | source)
XLA Modules:
  0.0 37.3 jit_solution(14599458803557637013)
XLA Ops:
  0.6 35.2 %shard_map.85 = (f32[1,32,6144]{2,1,0:T(8,128)S(1)}, f32[1,384]{1,0:T(1,128)S(1)}) custom-call(s32[1,2048]{1,0:T(1,128)} %node_ref.1, s32[1,2048]{1,0:T(1,128)} %wgt_ref.1, s32[1,32]{1,0:T(1,128)} %flag_ref.1, s32[2048,256]{1,0:T(8,128)} %bins_ref.1, f32[1,2048]{1,0:T(1,128)} %bitcast.2, f32[1,32,3072]{2,1,0:T(8,128)} %parent_ref.1), custom_call_target="tpu_custom_call" | custom-call | tf_op jit(solution)/shard_map/pallas_call | solution.py:401
  35.9 1.4 %shard_map.86 = (f32[1,32,6144]{2,1,0:T(8,128)}, f32[1,64]{1,0:T(1,128)}, f32[1,32]{1,0:T(1,128)}) custom-call(f32[1,32,6144]{2,1,0:T(8,128)S(1)} %get-tuple-element.8.child_in, f32[1,384]{1,0:T(1,128)S(1)} %get-tuple-element.9.small_in), custom_call_target="tpu_custom_call" | custom-call | tf_op jit(solution)/shard_map/pallas_call | solution.py:432

commit v2 on v1

--- a/solution.py
+++ b/solution.py
@@ -36,7 +36,7 @@
     R, T, owned, nbins, pairs, nrows,
     node_ref, wgt_ref, flag_ref, bins_ref, target_ref, parent_ref,
     child_ref, small_ref,
-    node_v, wgt_v, flag_v, bins_v, own_v, own_t, sendbuf, recv, stat_v, par_v, acc, spread, tn_v, sg_v,
+    node_v, wgt_v, target_v, flag_v, bins_v, own_v, own_t, sendbuf, recv, stat_v, par_v, acc, spread, tn_v, sg_v,
     msg_b, got_b, msg_i, got_i,
     in_sem, d_send, d_recv, s_send, s_recv, y_send, x_send, x_recv, p_send, p_recv, q_send, q_recv,
     b_send, b_recv, i_send, i_recv,
@@ -59,7 +59,7 @@
     bins_in.start()
     node_in = pltpu.make_async_copy(node_ref, node_v, in_sem.at[2])
     wgt_in = pltpu.make_async_copy(wgt_ref, wgt_v, in_sem.at[3])
-    target_in = pltpu.make_async_copy(target_ref, stat_v.at[r, :, pl.ds(2 * nrows, nrows)], in_sem.at[4])
+    target_in = pltpu.make_async_copy(target_ref, target_v, in_sem.at[4])
     node_in.start()
     wgt_in.start()
     target_in.start()
@@ -81,13 +81,20 @@
     node_in.wait()
     wgt_in.wait()
     target_in.wait()
-    stat_v[r, :, 0:nrows] = node_v[...].astype(f32)
-    stat_v[r, :, nrows : 2 * nrows] = wgt_v[...].astype(f32)
+    lines = nrows // 128
+    for n, held in enumerate((node_v, wgt_v, target_v)):
+        for i in range(lines):
+            stat_v[r, n * lines + i : n * lines + i + 1, :] = held[:, i * 128 : (i + 1) * 128].astype(f32)
     bins_in.wait()
     sendbuf[...] = bins_v[...].astype(f32).T.reshape(R, owned, quarter)
 
     def flip(m):
         peer, bit = r, 1
+        if isinstance(m, int):
+            while bit < R:
+                if m // bit % 2:
+                    peer = peer + bit * (1 - 2 * lax.rem(r // bit, 2))
+                bit *= 2
         while bit < R:
             on = lax.rem(m // bit, 2)
             peer = peer + on * bit * (1 - 2 * lax.rem(r // bit, 2))
@@ -121,15 +128,13 @@
 
     pl.semaphore_wait(barrier, R + T - 2)
 
-    def launch(m, _):
-        @pl.when((m == 1) | (lax.rem(m, 2) == 0))
-        def _():
-            stats_out(m).start()
-
+    stats_out(1).start()
+    for m in range(2, R, 2):
+        stats_out(m).start()
+
+    turns = [1, 2, 3] if R == 4 else [1, 2, 3, R - 2, R - 1, *range(4, R - 2)]
+    for m in turns:
         direct(m, r).start()
-        return 0
-
-    lax.fori_loop(1, R, launch, 0)
 
     for a in accs:
         acc[0] = pltpu.matmul_pop(a)
@@ -175,23 +180,21 @@
     third = lax.rem(lax.broadcasted_iota(i32, (48, quarter), 0), 3)
     count = R * T
 
+    lags = (0, 3, 1, 4)
+    plan = [(0, -1 - k) for k in range(T)]
+    for j in range(R - 1 + max(lags)):
+        plan += [(turns[j - lag], k) for k, lag in enumerate(lags) if 0 <= j - lag < R - 1]
+
     def place(e):
-        u = e - T
-        idx = u + jnp.where(u >= 1, 3, 0) + jnp.where(u >= 4, 1, 0)
-        idx = idx + jnp.where(u >= 4 * R - 8, 1, 0) + jnp.where(u >= 4 * R - 5, 3, 0)
-        k = lax.rem(idx, 4)
-        m = idx // 4 + 1 - (k + 1) // 2
-        m = jnp.where(e < T, 0, m)
-        slot = jnp.where(k == 0, t, jnp.where(k == 1, tx, jnp.where(k == 2, tp, tpx)))
-        slot = jnp.where(e < T, e, slot)
-        k = jnp.where(e < T, -1, k)
-        return m, k, slot
+        m, k = plan[e]
+        return m, k, (t, tx, tp, tpx)[k] if k >= 0 else -1 - k
 
     def lay(src, slot):
-        base = pl.multiple_of(slot * quarter, quarter)
-        nodes = stat_v[src, :, pl.ds(base, quarter)]
-        w = stat_v[src, :, pl.ds(pl.multiple_of(base + nrows, quarter), quarter)]
-        y = stat_v[src, :, pl.ds(pl.multiple_of(base + 2 * nrows, quarter), quarter)]
+        def line(n):
+            at = n * lines + slot * (quarter // 128)
+            return jnp.concatenate([stat_v[src, pl.ds(at + i, 1), :] for i in range(quarter // 128)], axis=1)
+
+        nodes, w, y = line(0), line(1), line(2)
         wy = w * y
         wyy = wy * y
         stat = jnp.where(third == 0, w, jnp.where(third == 1, wy, wyy)).astype(bf16)
@@ -233,16 +236,15 @@
         def _():
             relay(src, tpx, tp, q_send, q_recv).wait_recv()
 
-        m2, k2, slot2 = place(jnp.minimum(e + 1, count - 1))
+        m2, k2, slot2 = place(min(e + 1, count - 1))
         src2 = flip(m2)
 
-        @pl.when((k2 == 0) & (e + 1 < count))
-        def _():
+        if k2 == 0 and e + 1 < count and m2 % 2 == 1:
             stats(src2, src2, y_send).wait_recv()
-
-            @pl.when(lax.rem(m2, 2) == 0)
-            def _():
-                stats(src2, flip(1), y_send).start()
+            later = turns[turns.index(m2) + 1 :][:1]
+            for m in later:
+                stats(flip(m), flip(m), y_send).wait_recv()
+                stats(flip(m), flip(1), y_send).start()
 
         lay(src2, slot2)
         cols = recv[src, slot].astype(bf16)
@@ -263,7 +265,8 @@
                         stage(tile, q)
         return 0
 
-    lax.fori_loop(0, count, step, 0)
+    for e in range(count):
+        step(e, 0)
     nothing = jnp.zeros((16, 256), bf16)
     for tile in range(2):
         pltpu.matmul_acc_lhs(idle0, nothing, load_staged_rhs=tile)
@@ -406,13 +409,14 @@
         scratch_shapes=[
             pltpu.VMEM((1, nrows), jnp.int32),
             pltpu.VMEM((1, nrows), jnp.int32),
+            pltpu.VMEM((1, nrows), f32),
             pltpu.VMEM((1, pairs), jnp.int32),
             pltpu.VMEM((quarter, feat), jnp.int32),
             pltpu.VMEM((nrows, 128), jnp.int32),
             pltpu.VMEM((T, 128, quarter), f32),
             pltpu.VMEM((R, owned, quarter), f32),
             pltpu.VMEM((R, T, owned, quarter), f32),
-            pltpu.VMEM((R, 1, 3 * nrows), f32),
+            pltpu.VMEM((R, 3 * nrows // 128, 128), f32),
             pltpu.VMEM((1, owned, BINS * 3 * pairs), f32),
             pltpu.VMEM((4, BINS // 4 * owned, 256), f32),
             pltpu.VMEM((256, quarter), bf16),

time: 37.4 us -> 34.1 us (0.912)
  Pallas kernels: 36.6 us -> 33.3 us
    pallas_call x1, Pallas kernels: 35.2 us -> 31.9 us  [fused(): pl.pallas_call(functools.partial(kernel, R, T, owned, BINS, pairs, nrows)...]
where the time goes in v2:
time: 34.1 us; the launch traced here: 33.9 us
  Pallas kernels  33.3 us (98%)
  between operations  0.64 us (2%)
    pallas_call x1, Pallas kernels, fused(): pl.pallas_call(functools.partial(kernel, R, T, owned, BINS, pairs, nrows)...  31.9 us
    pallas_call x1, Pallas kernels, fused(): pl.pallas_call(functools.partial(finish, owned, pairs), out_shape=(jax.Sh...  1.4 us

profile of v2, /device:TPU:0, one launch (start us, length us, event | category | flops | bytes accessed | tf_op | source)
XLA Modules:
  0.0 33.9 jit_solution(15446953039373455765)
XLA Ops:
  0.6 31.9 %shard_map.85 = (f32[1,32,6144]{2,1,0:T(8,128)S(1)}, f32[1,384]{1,0:T(1,128)S(1)}) custom-call(s32[1,2048]{1,0:T(1,128)} %node_ref.1, s32[1,2048]{1,0:T(1,128)} %wgt_ref.1, s32[1,32]{1,0:T(1,128)} %flag_ref.1, s32[2048,256]{1,0:T(8,128)} %bins_ref.1, f32[1,2048]{1,0:T(1,128)} %bitcast.2, f32[1,32,3072]{2,1,0:T(8,128)} %parent_ref.1), custom_call_target="tpu_custom_call" | custom-call | tf_op jit(solution)/shard_map/pallas_call | solution.py:404
  32.5 1.4 %shard_map.86 = (f32[1,32,6144]{2,1,0:T(8,128)}, f32[1,64]{1,0:T(1,128)}, f32[1,32]{1,0:T(1,128)}) custom-call(f32[1,32,6144]{2,1,0:T(8,128)S(1)} %get-tuple-element.8.child_in, f32[1,384]{1,0:T(1,128)S(1)} %get-tuple-element.9.small_in), custom_call_target="tpu_custom_call" | custom-call | tf_op jit(solution)/shard_map/pallas_call | solution.py:436
